TPU v7x, 256 devices: a whole 4x4x8 slice. The times are simulated.
256 devices in a mesh: expert: 32 (over y, x, core), tensor: 8 (over z).
Axes of the slice: x: 4, y: 4, z: 8, core: 2. Of those that a mesh axis runs over, the one named last changes fastest.
Arguments:
- tokens: bfloat16 [32768, 1024], P(('expert', 'tensor')), may hold values from -6 to 6
- grad_out: bfloat16 [32768, 1024], P(('expert', 'tensor')), may hold values from -6 to 6
- expert_ids: int32 [32768, 2], P(('expert', 'tensor')), may hold values from 0 to 31, all different within a row; in each aligned block of 128 rows (0 to 127, 128 to 255, ...) at most 12 rows name the same one
- probs: float32 [32768, 2], P(('expert', 'tensor')), may hold values from 0.2 to 1
- w_gate: bfloat16 [32, 1024, 2048], P('expert', None, 'tensor'), may hold values from -0.1875 to 0.1875
- w_up: bfloat16 [32, 1024, 2048], P('expert', None, 'tensor'), may hold values from -0.1875 to 0.1875
- w_down: bfloat16 [32, 2048, 1024], P('expert', 'tensor'), may hold values from -0.125 to 0.125
Outputs:
- d_tokens: bfloat16 [32768, 1024], P(('expert', 'tensor'))
- d_probs: float32 [32768, 2], P(('expert', 'tensor'))
- d_w_gate: float32 [32, 1024, 2048], P('expert', None, 'tensor')
- d_w_up: float32 [32, 1024, 2048], P('expert', None, 'tensor')
- d_w_down: float32 [32, 2048, 1024], P('expert', 'tensor')
Inputs may be any that keep to these rules, and one draw needn't show every extreme that they name: `expert_ids`: the two experts of a token differ. In each aligned block of 128 rows (the rows of one device) no expert is named more than 12 times, and in some block one expert is named exactly 12 times.
All inputs are finite; a program needn't handle non-finite values.
Results may differ from a plain program's by a relative error of at most 0.015.
Values may be sent and summed in bfloat16 or wider, within the bound.
A program may use at most 128 MiB of HBM per device.

v0:
```python
import jax
import jax.numpy as jnp
from jax import lax
from jax.sharding import PartitionSpec as P


def block_positions(flat_ids, experts):
    onehot = (flat_ids[:, None] == jnp.arange(experts, dtype=jnp.int32)[None, :]).astype(jnp.int32)
    earlier = jnp.cumsum(onehot, axis=0) - onehot
    return jnp.sum(earlier * onehot, axis=1)


def slot_sources(slot_of, total_slots):
    entries = slot_of.shape[0]
    match = slot_of[None, :] == jnp.arange(total_slots, dtype=jnp.int32)[:, None]
    found = jnp.sum(jnp.where(match, jnp.arange(entries, dtype=jnp.int32)[None, :], 0), axis=1)
    filled = jnp.any(match, axis=1)
    return jnp.where(filled, found, entries)


def pack_rows(tokens, grad_out, prob_flat, source, picks):
    zero_row = jnp.zeros((1, tokens.shape[1]), tokens.dtype)
    token_rows = jnp.concatenate([tokens, zero_row], 0)
    grad_rows = jnp.concatenate([grad_out, zero_row], 0)
    prob_rows = jnp.concatenate([prob_flat, jnp.zeros((1,), prob_flat.dtype)], 0)
    row_index = source // picks
    return (
        jnp.take(token_rows, row_index, axis=0),
        jnp.take(grad_rows, row_index, axis=0),
        jnp.take(prob_rows, source, axis=0),
    )


def expert_backward(rows_in, rows_grad, rows_prob, gate_mat, up_mat, down_mat):
    gate_pre = jnp.dot(rows_in, gate_mat, preferred_element_type=jnp.float32)
    up_pre = jnp.dot(rows_in, up_mat, preferred_element_type=jnp.float32)
    sigmoid = jax.nn.sigmoid(gate_pre)
    swished = gate_pre * sigmoid
    hidden = swished * up_pre
    weight = rows_prob.astype(jnp.float32)[:, None]
    hidden_w = (weight * hidden).astype(jnp.bfloat16)
    contract_cols = (((1,), (1,)), ((), ()))
    contract_rows = (((0,), (0,)), ((), ()))
    act_raw = lax.dot_general(
        rows_grad, down_mat, contract_cols, preferred_element_type=jnp.float32
    )
    prob_part = jnp.sum(hidden * act_raw, axis=1)
    act_grad = weight * act_raw
    gate_grad = (act_grad * up_pre * sigmoid * (1.0 + gate_pre * (1.0 - sigmoid))).astype(
        jnp.bfloat16
    )
    up_grad = (act_grad * swished).astype(jnp.bfloat16)
    down_wgrad = lax.dot_general(
        hidden_w, rows_grad, contract_rows, preferred_element_type=jnp.float32
    )
    gate_wgrad = lax.dot_general(
        rows_in, gate_grad, contract_rows, preferred_element_type=jnp.float32
    )
    up_wgrad = lax.dot_general(rows_in, up_grad, contract_rows, preferred_element_type=jnp.float32)
    input_part = lax.dot_general(
        gate_grad, gate_mat, contract_cols, preferred_element_type=jnp.float32
    )
    input_part = input_part + lax.dot_general(
        up_grad, up_mat, contract_cols, preferred_element_type=jnp.float32
    )
    return (input_part, prob_part, gate_wgrad, up_wgrad, down_wgrad)


def per_device(tokens, grad_out, expert_ids, probs, w_gate, w_up, w_down):
    experts = lax.axis_size("expert") * w_gate.shape[0]
    tensor_size = lax.axis_size("tensor")
    own_rows = tokens.shape[0]
    picks = expert_ids.shape[1]
    width = tokens.shape[1]
    capacity = max(2, 3 * own_rows * picks // (2 * experts))
    gate_mat = w_gate[0]
    up_mat = w_up[0]
    down_mat = w_down[0]
    flat_ids = expert_ids.reshape(-1)
    own_slot = flat_ids * capacity + block_positions(flat_ids, experts)
    prob_b = probs.astype(jnp.bfloat16)
    all_in, all_grad, all_prob = (
        lax.all_gather(tokens, "tensor", axis=0, tiled=True),
        lax.all_gather(grad_out, "tensor", axis=0, tiled=True),
        lax.all_gather(prob_b, "tensor", axis=0, tiled=True),
    )
    all_ids = lax.all_gather(expert_ids, "tensor", axis=0, tiled=True)
    id_blocks = all_ids.reshape(tensor_size, own_rows * picks)

    def block_rank(block_ids):
        return block_positions(block_ids, experts)

    positions = jax.vmap(block_rank)(id_blocks)
    block_start = jnp.arange(tensor_size, dtype=jnp.int32)[:, None] * capacity
    slot_all = (id_blocks * (tensor_size * capacity) + block_start + positions).reshape(-1)
    source = slot_sources(slot_all, experts * tensor_size * capacity)
    send_in, send_grad, send_prob = pack_rows(all_in, all_grad, all_prob.reshape(-1), source, picks)
    rows_in, rows_grad, rows_prob = (
        lax.all_to_all(send_in, "expert", split_axis=0, concat_axis=0, tiled=True),
        lax.all_to_all(send_grad, "expert", split_axis=0, concat_axis=0, tiled=True),
        lax.all_to_all(send_prob, "expert", split_axis=0, concat_axis=0, tiled=True),
    )
    input_part, prob_part, gate_wgrad, up_wgrad, down_wgrad = expert_backward(
        rows_in, rows_grad, rows_prob, gate_mat, up_mat, down_mat
    )
    part_rows, part_probs = (
        lax.all_to_all(
            input_part.astype(jnp.bfloat16), "expert", split_axis=0, concat_axis=0, tiled=True
        ),
        lax.all_to_all(
            prob_part.astype(jnp.bfloat16), "expert", split_axis=0, concat_axis=0, tiled=True
        ),
    )
    part_rows = part_rows.reshape(experts, tensor_size, capacity, width).astype(jnp.float32)
    part_probs = part_probs.reshape(experts, tensor_size, capacity).astype(jnp.float32)
    summed_in, summed_prob = (
        lax.psum_scatter(
            part_rows.astype(jnp.bfloat16), "tensor", scatter_dimension=1, tiled=True
        ).astype(jnp.float32),
        lax.psum_scatter(
            part_probs.astype(jnp.bfloat16), "tensor", scatter_dimension=1, tiled=True
        ).astype(jnp.float32),
    )
    back_in = summed_in.reshape(experts * capacity, width)
    back_prob = summed_prob.reshape(experts * capacity)
    chosen = jnp.take(back_in, own_slot, axis=0).reshape(own_rows, picks, width)
    d_tokens = jnp.sum(chosen, axis=1).astype(jnp.bfloat16)
    d_probs = jnp.take(back_prob, own_slot, axis=0).reshape(own_rows, picks)
    return (d_tokens, d_probs, gate_wgrad[None], up_wgrad[None], down_wgrad[None])


def solution(mesh):
    return jax.shard_map(
        per_device,
        mesh=mesh,
        in_specs=(
            P(("expert", "tensor"), None),
            P(("expert", "tensor"), None),
            P(("expert", "tensor"), None),
            P(("expert", "tensor"), None),
            P("expert", None, "tensor"),
            P("expert", None, "tensor"),
            P("expert", "tensor", None),
        ),
        out_specs=(
            P(("expert", "tensor"), None),
            P(("expert", "tensor"), None),
            P("expert", None, "tensor"),
            P("expert", None, "tensor"),
            P("expert", "tensor", None),
        ),
        check_vma=False,
    )
```

profile of v0, /device:TPU:1, one launch (start us, length us, event | category | flops | bytes accessed | tf_op | source)
XLA Modules:
  0.0 488.9 jit_solution(18044483592733750279)
XLA Ops:
  7.2 0.7 all-gather.5.cloned.1.call-update
  8.0 0.7 all-gather.3.cloned.1.call-update
  8.7 16.7 %all_gather.12 = s32[1024,2]{0,1:T(2,128)S(1)} all-gather(s32[128,2]{0,1:T(2,128)} %param.11), channel_id=1, replica_groups=mesh['expert'=32,'tensor'=8] {'tensor'}, dimensions={0}, use_global_device_ids=true | all-gather | bytes 9216 | tf_op jit(solution)/shard_map/all_gather | solution.py:87
  25.6 0.3 eq.72
  26.3 0.7 convert_element_type.65
  27.0 10.6 %all_gather.13 = bf16[1024,2]{0,1:T(2,128)(2,1)S(1)} all-gather(bf16[128,2]{0,1:T(2,128)(2,1)S(1)} %convert_element_type.65), channel_id=1, replica_groups=mesh['expert'=32,'tensor'=8] {'tensor'}, dimensions={0}, use_global_device_ids=true | all-gather | bytes 4608 | tf_op jit(solution)/shard_map/all_gather | solution.py:85
  37.8 0.3 reshape.246
  38.1 4.6 reduce-window.16
  43.8 3.1 fusion
  46.9 2.6 select_reduce_fusion
  49.7 19.4 %gather_fusion = bf16[3072]{0:T(1024)(128)(2,1)S(1)} fusion(bf16[2049]{0:T(1024)(128)(2,1)S(1)} %pad_maximum_fusion, s32[3072]{0:T(1024)S(1)} %broadcast_clamp_fusion.1), kind=kCustom, calls=%fused_computation.2 | custom fusion | bytes 24576 | tf_op jit(solution)/shard_map/jit(_take)/gather | solution.py:30
  69.1 0.6 copy.59
  69.8 14.0 %all-to-all-start = ((bf16[32,96,1]{1,2,0:T(2,128)(2,1)}), bf16[32,96,1]{1,2,0:T(2,128)(2,1)S(1)}, u32[]{:S(2)}, u32[]{:S(2)}) async-start(bf16[32,96,1]{1,2,0:T(2,128)(2,1)} %copy.59), calls=%async_computation | async-start | bytes 32768 | tf_op jit(solution)/shard_map/all_to_all | solution.py:101
  83.8 1.8 concatenate.11
  85.6 13.9 %gather_fusion.4 = bf16[3072,1024]{1,0:T(8,128)(2,1)} fusion(bf16[1025,1024]{1,0:T(8,128)(2,1)S(1)} %concatenate.11, s32[3072]{0:T(1024)S(1)} %broadcast_clamp_fusion), kind=kCustom, calls=%fused_computation.1.clone | custom fusion | bytes 12595200 | tf_op jit(solution)/shard_map/jit(_take)/gather | solution.py:28
  99.5 1.8 concatenate.10
  101.3 14.0 %gather_fusion.3 = bf16[3072,1024]{1,0:T(8,128)(2,1)} fusion(bf16[1025,1024]{1,0:T(8,128)(2,1)S(1)} %concatenate.10, s32[3072]{0:T(1024)S(1)} %broadcast_clamp_fusion), kind=kCustom, calls=%fused_computation.clone | custom fusion | bytes 12595200 | tf_op jit(solution)/shard_map/jit(_take)/gather | solution.py:29
  115.3 10.4 %broadcast_select_fusion.1 = (bf16[3072,1024]{1,0:T(8,128)(2,1)}, bf16[3072,1024]{1,0:T(8,128)(2,1)}) fusion(bf16[3072,1024]{1,0:T(8,128)(2,1)} %gather_fusion.3, pred[3072]{0:T(1024)(128)(4,1)S(1)} %get-tuple-element.23, bf16[3072,1024]{1,0:T(8,128)(2,1)} %gather_fusion.4), kind=kLoop, calls=%fused_computation.10 | loop fusion | flops 6291456 | bytes 25168896 | tf_op jit(solution)/shard_map/jit(_take)/select_n | solution.py:29
  125.6 80.7 %all_to_all.45 = bf16[32,96,1024]{2,1,0:T(8,128)(2,1)} all-to-all(bf16[32,96,1024]{2,1,0:T(8,128)(2,1)} %bitcast.96), channel_id=1, replica_groups=mesh['expert'=32,'tensor'=8] {'expert'}, dimensions={0} | all-to-all | bytes 12582912 | tf_op jit(solution)/shard_map/all_to_all | solution.py:99
  206.3 5.4 %all-to-all-start.1 = ((bf16[32,96,1024]{2,1,0:T(8,128)(2,1)}), bf16[32,96,1024]{2,1,0:T(8,128)(2,1)}, u32[]{:S(2)}, u32[]{:S(2)}) async-start(bf16[32,96,1024]{2,1,0:T(8,128)(2,1)} %bitcast.95), calls=%async_computation.1 | async-start | bytes 12582912 | tf_op jit(solution)/shard_map/all_to_all | solution.py:100
  211.9 6.5 %fusion.8 = f32[3072,256]{0,1:T(8,128)} fusion(bf16[3072,1024]{1,0:T(8,128)(2,1)} %bitcast.97, bf16[1,1024,256]{2,1,0:T(8,128)(2,1)S(1)} %copy-done), kind=kOutput, calls=%fused_computation.26 | convolution fusion | flops 1610612736 | bytes 9961472 | tf_op jit(solution)/shard_map/dot_general | solution.py:35
  218.4 3.6 fusion.11
  222.0 62.7 %all-to-all-done.1 = bf16[32,96,1024]{2,1,0:T(8,128)(2,1)} async-done(((bf16[32,96,1024]{2,1,0:T(8,128)(2,1)}), bf16[32,96,1024]{2,1,0:T(8,128)(2,1)}, u32[]{:S(2)}, u32[]{:S(2)}) %all-to-all-start.1) | async-done | bytes 6291488 | tf_op jit(solution)/shard_map/all_to_all | solution.py:100
  284.7 9.0 %multiply_reduce_fusion = (bf16[3072]{0:T(1024)(128)(2,1)S(1)}, bf16[3072,256]{0,1:T(8,128)(2,1)S(1)}, bf16[3072,256]{0,1:T(8,128)(2,1)}) fusion(f32[3072,256]{0,1:T(8,128)} %fusion.11, f32[3072,256]{0,1:T(8,128)} %fusion.8, f32[3072]{0:T(1024)S(1)} %reshape.253, bf16[3072,1024]{1,0:T(8,128)(2,1)} %bitcast.6, bf16[1,256,1024]{2,1,0:T(8,128)(2,1)} %param.15), kind=kOutput, calls=%fused_computation.12 | convolution fusion | flops 1623979008 | bytes 16271360 | tf_op jit(solution)/shard_map/dot_general | solution.py:44
  293.7 0.8 convert_element_type.76
  294.5 8.5 %all-to-all-start.4 = ((bf16[32,96,1]{1,2,0:T(2,128)(2,1)}), bf16[32,96,1]{1,2,0:T(2,128)(2,1)S(1)}, u32[]{:S(2)}, u32[]{:S(2)}) async-start(bf16[32,96,1]{1,2,0:T(2,128)(2,1)} %convert_element_type.76), calls=%async_computation.5 | async-start | bytes 32768 | tf_op jit(solution)/shard_map/all_to_all | solution.py:110
  303.1 1.9 fusion.6
  305.0 4.5 add_convert_fusion
  309.5 0.6 all-to-all-done.4
  310.1 7.0 %all-to-all-start.3 = ((bf16[32,96,1024]{2,1,0:T(8,128)(2,1)}), bf16[32,96,1024]{2,1,0:T(8,128)(2,1)}, u32[]{:S(2)}, u32[]{:S(2)}) async-start(bf16[32,96,1024]{2,1,0:T(8,128)(2,1)} %bitcast.94), calls=%async_computation.3 | async-start | bytes 12582912 | tf_op jit(solution)/shard_map/all_to_all | solution.py:107
  317.2 0.6 reshape.250
  318.1 72.6 %all-to-all-done.3 = bf16[32,96,1024]{2,1,0:T(8,128)(2,1)} async-done(((bf16[32,96,1024]{2,1,0:T(8,128)(2,1)}), bf16[32,96,1024]{2,1,0:T(8,128)(2,1)}, u32[]{:S(2)}, u32[]{:S(2)}) %all-to-all-start.3) | async-done | bytes 6291488 | tf_op jit(solution)/shard_map/all_to_all | solution.py:107
  390.7 8.9 %copy.60 = bf16[32,96,1024]{2,0,1:T(8,128)(2,1)} copy(bf16[32,96,1024]{2,1,0:T(8,128)(2,1)} %all-to-all-done.3) | data formatting | bytes 12582912 | tf_op jit(solution)/shard_map/all_to_all | solution.py:107
  399.6 0.7 copy-done.5
  400.7 0.6 reduce-window.14
  402.0 6.2 %convolution_bitcast_fusion.1 = f32[1,1024,256]{2,1,0:T(8,128)} fusion(bf16[3072,1024]{1,0:T(8,128)(2,1)} %bitcast.98, bf16[3072,256]{0,1:T(8,128)(2,1)} %copy-done.1), kind=kOutput, calls=%fused_computation.22 | convolution fusion | flops 1610612736 | bytes 8912896 | tf_op jit(solution)/shard_map/dot_general | solution.py:56
  408.2 2.9 convolution_bitcast_fusion
  411.1 0.9 copy-done.7
  411.9 5.7 %fusion.5 = f32[1,256,1024]{2,1,0:T(8,128)} fusion(bf16[3072,1024]{1,0:T(8,128)(2,1)} %bitcast.6, f32[3072]{0:T(1024)S(1)} %reshape.253, f32[3072,256]{0,1:T(8,128)S(1)} %copy-done.7, f32[3072,256]{0,1:T(8,128)S(1)} %copy-done.6), kind=kOutput, calls=%fused_computation.20 | convolution fusion | flops 1616117760 | bytes 13643776 | tf_op jit(solution)/shard_map/dot_general | solution.py:53
  417.6 0.8 copy.64
  418.5 1.9 gather_fusion.2
  420.6 0.6 copy.65
  421.2 52.3 %reduce-scatter.3.cloned.1.call-done = bf16[32,1,12,1024]{3,0,2,1:T(8,128)(2,1)} async-done(((bf16[32,8,12,1024]{3,0,2,1:T(8,128)(2,1)}), bf16[32,1,12,1024]{3,0,2,1:T(8,128)(2,1)}) %reduce-scatter.3.cloned.1.call-update) | async-done | bytes 786448 | tf_op jit(solution)/shard_map/reduce_scatter | solution.py:117
  473.5 3.0 copy.61
  476.5 1.6 reshape.255
  478.1 1.1 gather_fusion.1
  479.2 0.6 gather.24
  479.8 2.2 select_reduce_fusion.1
  (79 shorter events, 4.0 us)
Async XLA Ops:
  7.2 204.7 %copy-start = (bf16[1,1024,256]{2,1,0:T(8,128)(2,1)S(1)}, bf16[1,1024,256]{2,1,0:T(8,128)(2,1)}, u32[]{:S(2)}) copy-start(bf16[1,1024,256]{2,1,0:T(8,128)(2,1)} %param.13) | copy-start | bytes 1572868
  7.2 76.6 %all-gather.5.cloned.1.call-start = ((), (), s32[]{:S(2)}) async-start(), calls=%async_computation.8 | async-start | bytes 2359296 | tf_op jit(solution)/shard_map/all_gather | solution.py:83
  7.9 91.6 %all-gather.3.cloned.1.call-start = ((), (), s32[]{:S(2)}) async-start(), calls=%async_computation.7 | async-start | bytes 2359296 | tf_op jit(solution)/shard_map/all_gather | solution.py:84
  69.8 55.9 %all-to-all-start = ((bf16[32,96,1]{1,2,0:T(2,128)(2,1)}), bf16[32,96,1]{1,2,0:T(2,128)(2,1)S(1)}, u32[]{:S(2)}, u32[]{:S(2)}) async-start(bf16[32,96,1]{1,2,0:T(2,128)(2,1)} %copy.59), calls=%async_computation | async-start | bytes 32768 | tf_op jit(solution)/shard_map/all_to_all | solution.py:101
  206.3 12.1 %slice-start = ((s8[6291456]{0:T(1024)(128)(4,1)}), s8[2097152]{0:T(1024)(128)(4,1)S(1)}, s32[]{:S(2)}) async-start(s8[6291456]{0:T(1024)(128)(4,1)} %bitcast.99), calls=%async_computation.11 | async-start | bytes 4194304
  206.3 78.4 %all-to-all-start.1 = ((bf16[32,96,1024]{2,1,0:T(8,128)(2,1)}), bf16[32,96,1024]{2,1,0:T(8,128)(2,1)}, u32[]{:S(2)}, u32[]{:S(2)}) async-start(bf16[32,96,1024]{2,1,0:T(8,128)(2,1)} %bitcast.95), calls=%async_computation.1 | async-start | bytes 12582912 | tf_op jit(solution)/shard_map/all_to_all | solution.py:100
  211.8 6.6 %slice-start.1 = ((s8[6291456]{0:T(1024)(128)(4,1)}), s8[4194304]{0:T(1024)(128)(4,1)S(1)}, s32[]{:S(2)}) async-start(s8[6291456]{0:T(1024)(128)(4,1)} %bitcast.99), calls=%async_computation.12 | async-start | bytes 8388608
  211.8 6.6 %copy-start.4 = (bf16[1,1024,256]{2,1,0:T(8,128)(2,1)S(1)}, bf16[1,1024,256]{2,1,0:T(8,128)(2,1)}, u32[]{:S(2)}) copy-start(bf16[1,1024,256]{2,1,0:T(8,128)(2,1)} %param.14) | copy-start | bytes 1572868
  293.7 11.2 %copy-start.1 = (bf16[3072,256]{0,1:T(8,128)(2,1)}, bf16[3072,256]{0,1:T(8,128)(2,1)S(1)}, u32[]{:S(2)}) copy-start(bf16[3072,256]{0,1:T(8,128)(2,1)S(1)} %get-tuple-element.26) | copy-start | bytes 4718596
  294.5 15.5 %all-to-all-start.4 = ((bf16[32,96,1]{1,2,0:T(2,128)(2,1)}), bf16[32,96,1]{1,2,0:T(2,128)(2,1)S(1)}, u32[]{:S(2)}, u32[]{:S(2)}) async-start(bf16[32,96,1]{1,2,0:T(2,128)(2,1)} %convert_element_type.76), calls=%async_computation.5 | async-start | bytes 32768 | tf_op jit(solution)/shard_map/all_to_all | solution.py:110
  303.1 1.9 copy-start.2
  310.1 80.6 %all-to-all-start.3 = ((bf16[32,96,1024]{2,1,0:T(8,128)(2,1)}), bf16[32,96,1024]{2,1,0:T(8,128)(2,1)}, u32[]{:S(2)}, u32[]{:S(2)}) async-start(bf16[32,96,1024]{2,1,0:T(8,128)(2,1)} %bitcast.94), calls=%async_computation.3 | async-start | bytes 12582912 | tf_op jit(solution)/shard_map/all_to_all | solution.py:107
  317.1 100.5 %reduce-scatter.5.cloned.1.call-start = ((), (), s32[]{:S(2)}) async-start(), calls=%async_computation.10 | async-start | bytes 36864 | tf_op jit(solution)/shard_map/reduce_scatter | solution.py:120
  317.9 155.6 %reduce-scatter.3.cloned.1.call-start = ((), (), s32[]{:S(2)}) async-start(), calls=%async_computation.9 | async-start | bytes 7077888 | tf_op jit(solution)/shard_map/reduce_scatter | solution.py:117
  399.6 0.7 copy-start.5
  399.6 8.6 %slice-start.2 = ((s8[6291456]{0:T(1024)(128)(4,1)}), s8[2097152]{0:T(1024)(128)(4,1)S(1)}, s32[]{:S(2)}) async-start(s8[6291456]{0:T(1024)(128)(4,1)} %bitcast.102), calls=%async_computation.13 | async-start | bytes 4194304
  401.9 6.2 %slice-start.3 = ((s8[6291456]{0:T(1024)(128)(4,1)}), s8[4194304]{0:T(1024)(128)(4,1)S(1)}, s32[]{:S(2)}) async-start(s8[6291456]{0:T(1024)(128)(4,1)} %bitcast.102), calls=%async_computation.14 | async-start | bytes 8388608
  402.0 6.2 %copy-start.3 = (bf16[3072,256]{0,1:T(8,128)(2,1)S(1)}, bf16[3072,256]{0,1:T(8,128)(2,1)}, u32[]{:S(2)}) copy-start(bf16[3072,256]{0,1:T(8,128)(2,1)} %get-tuple-element.27) | copy-start | bytes 4718596
  408.2 2.9 copy-start.6
  408.2 3.7 copy-start.7
Sparse Core Ops, SparseCore 0:
  9.8 40.4 all-gather.4
  52.0 39.5 all-gather.2
  320.9 31.9 reduce-scatter.4
  399.7 73.7 reduce-scatter.2
where the time goes:
time: 498 us; the launch traced here: 489 us
  waiting for transfers between devices  190 us (38%)
  blocking collectives  108 us (22%)
  local copies, waits for them, and re-layouts  76.6 us (15%)
  matrix products  40.2 us (8%)
  starting transfers between devices  35.2 us (7%)
  other arithmetic  24.7 us (5%)
  between operations  14.5 us (3%)
    all_to_all x1, blocking collectives, per_device(): lax.all_to_all(send_in, 'expert', split_axis=0, concat_axis=0, tiled=True)  80.7 us
    all_to_all x1, waiting for transfers between devices, per_device(): lax.all_to_all(input_part.astype(jnp.bfloat16), 'expert', split_axis=0, c...  72.6 us
    all_to_all x1, waiting for transfers between devices, per_device(): lax.all_to_all(send_grad, 'expert', split_axis=0, concat_axis=0, tiled=True)  62.7 us
    reduce_scatter x1, waiting for transfers between devices, per_device(): lax.psum_scatter(part_rows.astype(jnp.bfloat16), 'tensor', scatter_dimens...  52.3 us
    gather x2, local copies, waits for them, and re-layouts, pack_rows(): jnp.take(prob_rows, source, axis=0)  19.4 us
    all_gather x1, blocking collectives, per_device(): all_ids = lax.all_gather(expert_ids, 'tensor', axis=0, tiled=True)  16.7 us
    gather x1, local copies, waits for them, and re-layouts, pack_rows(): jnp.take(grad_rows, row_index, axis=0)  14 us
    all_to_all x1, starting transfers between devices, per_device(): lax.all_to_all(send_prob, 'expert', split_axis=0, concat_axis=0, tiled=True)  14 us
  transfers between devices with their start and end apart: 8, of which 4 were waited for; matrix products, arithmetic and copies ran while one was open for 25% of the time, Pallas kernels for 0%

commit v1 on v0

v1 whole, which is shorter than its diff:
```python
import jax
import jax.numpy as jnp
from jax import lax
from jax.sharding import PartitionSpec as P

F32 = jnp.float32
BF16 = jnp.bfloat16


def dot(a, b, ca, cb):
    return lax.dot_general(a, b, (((ca,), (cb,)), ((), ())), preferred_element_type=F32)


def slot_masks(ids, experts, capacity):
    rows = ids.shape[1]
    lane = jnp.arange(experts, dtype=jnp.int32)[:, None]
    hot = [(lane == ids[j][None, :]).astype(BF16) for j in range(ids.shape[0])]
    order = jnp.arange(rows, dtype=jnp.int32)
    before = (order[:, None] < order[None, :]).astype(BF16)
    earlier = dot(hot[0] + hot[1], before, 1, 0)
    slots = jnp.arange(experts * capacity, dtype=jnp.int32)[:, None]
    masks = []
    for j in range(ids.shape[0]):
        place = jnp.sum(hot[j].astype(F32) * earlier, axis=0).astype(jnp.int32)
        masks.append(slots == (ids[j] * capacity + place)[None, :])
    return masks


def expert_backward(rows_in, rows_grad, gate_mat, up_mat, down_mat):
    gate_pre = dot(rows_in, gate_mat, 1, 0)
    up_pre = dot(rows_in, up_mat, 1, 0)
    sigmoid = jax.nn.sigmoid(gate_pre)
    swished = gate_pre * sigmoid
    hidden = swished * up_pre
    act = dot(rows_grad, down_mat, 1, 1)
    prob_part = jnp.sum(hidden * act, axis=1)
    gate_grad = (act * up_pre * sigmoid * (1.0 + gate_pre * (1.0 - sigmoid))).astype(BF16)
    up_grad = (act * swished).astype(BF16)
    input_part = dot(gate_grad, gate_mat, 1, 1) + dot(up_grad, up_mat, 1, 1)
    down_wgrad = dot(hidden.astype(BF16), rows_grad, 0, 0)
    gate_wgrad = dot(rows_in, gate_grad, 0, 0)
    up_wgrad = dot(rows_in, up_grad, 0, 0)
    return input_part.astype(BF16), prob_part, gate_wgrad, up_wgrad, down_wgrad


def per_device(tokens, grad_out, expert_ids, probs, w_gate, w_up, w_down):
    experts = lax.axis_size("expert") * w_gate.shape[0]
    own_rows = tokens.shape[0]
    picks = expert_ids.shape[1]
    capacity = max(2, 3 * own_rows * picks // (2 * experts))
    masks = slot_masks(expert_ids.T, experts, capacity)
    prob_b = probs.astype(BF16).T
    pick_of = sum(m.astype(BF16) for m in masks)
    weight_of = sum(jnp.where(masks[j], prob_b[j][None, :], 0) for j in range(picks))
    send_in = dot(pick_of, tokens, 1, 0).astype(BF16)
    send_grad = dot(weight_of, grad_out, 1, 0).astype(BF16)

    def exchange(a):
        return lax.all_to_all(a, "expert", split_axis=0, concat_axis=0, tiled=True)

    rows_in = lax.all_gather(exchange(send_in), "tensor", axis=0, tiled=True)
    rows_grad = lax.all_gather(exchange(send_grad), "tensor", axis=0, tiled=True)
    input_part, prob_part, gate_wgrad, up_wgrad, down_wgrad = expert_backward(
        rows_in, rows_grad, w_gate[0], w_up[0], w_down[0]
    )
    back_prob = exchange(lax.psum_scatter(prob_part, "tensor", scatter_dimension=0, tiled=True))
    back_in = exchange(lax.psum_scatter(input_part, "tensor", scatter_dimension=0, tiled=True))
    d_tokens = dot(pick_of, back_in, 0, 0).astype(BF16)
    d_probs = jnp.stack(
        [jnp.sum(jnp.where(m, back_prob[:, None], 0.0), axis=0) for m in masks], axis=1
    )
    d_probs = d_probs / prob_b.T.astype(F32)
    return (d_tokens, d_probs, gate_wgrad[None], up_wgrad[None], down_wgrad[None])


def solution(mesh):
    rows = P(("expert", "tensor"), None)
    cols = P("expert", None, "tensor")
    down = P("expert", "tensor", None)
    return jax.shard_map(
        per_device,
        mesh=mesh,
        in_specs=(rows, rows, rows, rows, cols, cols, down),
        out_specs=(rows, rows, cols, cols, down),
        check_vma=False,
    )
```

time: 498 us -> 311 us (0.62); the launches traced: 489 us -> 310 us
  local copies, waits for them, and re-layouts: 76.6 us -> 8.21 us
  waiting for transfers between devices: 190 us -> 147 us
  blocking collectives: 108 us -> 69.4 us
  other arithmetic: 24.7 us -> 2.17 us
  starting transfers between devices: 35.2 us -> 21.8 us
  matrix products: 40.2 us -> 47.1 us
    all_to_all x4 -> x2, waiting for transfers between devices: 136 us -> 9.42 us  [exchange(): return lax.all_to_all(a, 'expert', split_axis=0, concat_axis=0, tiled=True)]
    all_gather x2, waiting for transfers between devices: 0.02 us -> 116 us  [the longest x1 65.4 us: per_device(): lax.all_gather(exchange(send_grad), 'tensor', axis=0, tiled=True)]
    gather x8 -> x0, local copies, waits for them, and re-layouts: 51.1 us -> none  [the longest x2 19.4 us: pack_rows(): jnp.take(prob_rows, source, axis=0)]
    all_to_all x1 -> x2, blocking collectives: 80.7 us -> 46.1 us  [exchange(): return lax.all_to_all(a, 'expert', split_axis=0, concat_axis=0, tiled=True)]
    reduce_scatter x2 -> x1, waiting for transfers between devices: 52.3 us -> 21.2 us  [per_device(): lax.psum_scatter(input_part, 'tensor', scatter_dimension=0, tiled=True)]
    all_gather x2 -> x0, blocking collectives: 27.3 us -> none  [the longest x1 16.7 us: per_device(): all_ids = lax.all_gather(expert_ids, 'tensor', axis=0, tiled=True)]
    unnamed x0 -> x1, blocking collectives: none -> 23.4 us
    all_to_all x4 -> x2, starting transfers between devices: 34.8 us -> 21.5 us  [exchange(): return lax.all_to_all(a, 'expert', split_axis=0, concat_axis=0, tiled=True)]
  transfers between devices with their start and end apart: 8 -> 5, of which waited for: 4 -> 4; matrix products, arithmetic and copies ran while one was open for 25% -> 10% of each run, Pallas kernels for 0% -> 0%
where the time goes in v1:
time: 311 us; the launch traced here: 310 us
  waiting for transfers between devices  147 us (47%)
  blocking collectives  69.4 us (22%)
  matrix products  47.1 us (15%)
  starting transfers between devices  21.8 us (7%)
  between operations  14.6 us (5%)
  local copies, waits for them, and re-layouts  8.21 us (3%)
    all_gather x1, waiting for transfers between devices, per_device(): lax.all_gather(exchange(send_grad), 'tensor', axis=0, tiled=True)  65.4 us
    all_gather x1, waiting for transfers between devices, per_device(): rows_in = lax.all_gather(exchange(send_in), 'tensor', axis=0, tiled=True)  50.8 us
    dot_general x12, matrix products, dot(): lax.dot_general(a, b, (((ca,), (cb,)), ((), ())), preferred_element_type=...  47.1 us
    all_to_all x2, blocking collectives, exchange(): return lax.all_to_all(a, 'expert', split_axis=0, concat_axis=0, tiled=True)  46.1 us
    unnamed x1, blocking collectives  23.4 us
    all_to_all x2, starting transfers between devices, exchange(): return lax.all_to_all(a, 'expert', split_axis=0, concat_axis=0, tiled=True)  21.5 us
    reduce_scatter x1, waiting for transfers between devices, per_device(): lax.psum_scatter(input_part, 'tensor', scatter_dimension=0, tiled=True)  21.2 us
    all_to_all x2, waiting for transfers between devices, exchange(): return lax.all_to_all(a, 'expert', split_axis=0, concat_axis=0, tiled=True)  9.42 us
  transfers between devices with their start and end apart: 5, of which 4 were waited for; matrix products, arithmetic and copies ran while one was open for 10% of the time, Pallas kernels for 0%

profile of v1, /device:TPU:1, one launch (start us, length us, event | category | flops | bytes accessed | tf_op | source)
XLA Modules:
  0.0 310.2 jit_solution(14581573565148855879)
XLA Ops:
  7.2 0.0 copy-start
  7.2 0.0 all-gather.5.cloned.1.call-start
  7.2 0.8 slice_bitcast_fusion.3
  8.0 0.2 multiply_reduce_fusion.2
  8.1 0.8 fusion.43
  8.9 1.3 convolution_convert_fusion
  10.2 0.0 copy-start.5
  10.2 0.0 copy-start.4
  10.2 0.2 all_to_all.33
  10.4 25.4 %all_to_all.45 = bf16[32,12,1024]{2,1,0:T(8,128)(2,1)S(1)} all-to-all(bf16[32,12,1024]{2,1,0:T(8,128)(2,1)S(1)} %all_to_all.33), channel_id=1, replica_groups=mesh['expert'=32,'tensor'=8] {'expert'}, dimensions={0} | all-to-all | bytes 1572864 | tf_op jit(solution)/shard_map/all_to_all | solution.py:59
  35.8 1.1 all_to_all.35
  36.9 0.0 all-gather.5.cloned.1.call-update
  36.9 0.0 all-gather.3.cloned.1.call-start
  37.0 0.4 convolution_convert_fusion.1
  37.4 0.2 all_to_all.30
  37.6 20.7 %all_to_all.46 = bf16[32,12,1024]{2,1,0:T(8,128)(2,1)S(1)} all-to-all(bf16[32,12,1024]{2,1,0:T(8,128)(2,1)S(1)} %all_to_all.30), channel_id=1, replica_groups=mesh['expert'=32,'tensor'=8] {'expert'}, dimensions={0} | all-to-all | bytes 1572864 | tf_op jit(solution)/shard_map/all_to_all | solution.py:59
  58.2 1.1 all_to_all.32
  59.3 0.0 all-gather.3.cloned.1.call-update
  59.3 0.0 copy-start.3
  59.3 0.2 reduce-scatter.2.cloned.1.call-start
  59.5 50.8 %all-gather.5.cloned.1.call-done = bf16[3072,1024]{1,0:T(8,128)(2,1)} async-done(((bf16[384,1024]{1,0:T(8,128)(2,1)}), bf16[3072,1024]{1,0:T(8,128)(2,1)}) %all-gather.5.cloned.1.call-update) | async-done | bytes 6291472 | tf_op jit(solution)/shard_map/all_gather | solution.py:61
  110.4 6.4 %fusion.9 = f32[3072,256]{0,1:T(8,128)} fusion(bf16[3072,1024]{1,0:T(8,128)(2,1)} %all-gather.5.cloned.1.call-done, bf16[1,1024,256]{2,1,0:T(8,128)(2,1)S(1)} %copy-done), kind=kOutput, calls=%fused_computation.17 | convolution fusion | flops 1610612736 | bytes 9961472 | tf_op jit(solution)/shard_map/dot_general | solution.py:11
  116.8 3.6 %fusion.12 = f32[3072,256]{0,1:T(8,128)} fusion(bf16[3072,1024]{1,0:T(8,128)(2,1)S(1)} %copy-done.6, bf16[1,1024,256]{2,1,0:T(8,128)(2,1)S(1)} %copy-done.3), kind=kOutput, calls=%fused_computation.20 | convolution fusion | flops 1610612736 | bytes 9961472 | tf_op jit(solution)/shard_map/dot_general | solution.py:11
  120.4 65.4 %all-gather.3.cloned.1.call-done = bf16[3072,1024]{1,0:T(8,128)(2,1)} async-done(((bf16[384,1024]{1,0:T(8,128)(2,1)}), bf16[3072,1024]{1,0:T(8,128)(2,1)}) %all-gather.3.cloned.1.call-update) | async-done | bytes 6291472 | tf_op jit(solution)/shard_map/all_gather | solution.py:62
  185.8 9.0 %multiply_reduce_fusion = (f32[3072]{0:T(1024)S(1)}, bf16[3072,256]{0,1:T(8,128)(2,1)S(1)}, bf16[3072,256]{0,1:T(8,128)(2,1)S(1)}) fusion(f32[3072,256]{0,1:T(8,128)} %fusion.12, f32[3072,256]{0,1:T(8,128)} %fusion.9, bf16[3072,1024]{1,0:T(8,128)(2,1)} %all-gather.3.cloned.1.call-done, bf16[1,256,1024]{2,1,0:T(8,128)(2,1)S(1)} %copy-done.7), kind=kOutput, calls=%fused_computation.1 | convolution fusion | flops 1623192576 | bytes 16265216 | tf_op jit(solution)/shard_map/dot_general | solution.py:11
  194.8 1.9 fusion.7
  196.7 4.5 %add_convert_fusion = bf16[3072,1024]{1,0:T(8,128)(2,1)} fusion(f32[3072,1024]{1,0:T(8,128)S(1)} %fusion.7, bf16[3072,256]{0,1:T(8,128)(2,1)S(1)} %get-tuple-element.11, bf16[1,1024,256]{2,1,0:T(8,128)(2,1)S(1)} %copy-done.3), kind=kOutput, calls=%fused_computation | convolution fusion | flops 1616904192 | bytes 20971520 | tf_op jit(solution)/shard_map/dot_general | solution.py:11
  201.2 0.0 reduce-scatter.2.cloned.1.call-update
  201.2 0.6 copy-done.8
  201.9 0.6 dynamic-slice
  203.1 23.4 %all-reduce = f32[3072]{0:T(1024)S(1)} all-reduce(f32[3072]{0:T(1024)S(1)} %get-tuple-element.9), channel_id=3, replica_groups=mesh['expert'=32,'tensor'=8] {'tensor'}, use_global_device_ids=true, to_apply=%region_4.5.clone | all-reduce | flops 3072 | bytes 24576
  226.4 0.1 dynamic-slice.1
  226.5 0.7 all_to_all.39
  227.2 13.9 %all-to-all-start.3 = ((f32[32,12,1]{1,2,0:T(1,128)}), f32[32,12,1]{1,2,0:T(1,128)S(1)}, u32[]{:S(2)}, u32[]{:S(2)}) async-start(f32[32,12,1]{1,2,0:T(1,128)} %bitcast.13), calls=%async_computation.4 | async-start | bytes 32768 | tf_op jit(solution)/shard_map/all_to_all | solution.py:59
  241.1 7.7 %fusion.4 = f32[1,256,1024]{2,1,0:T(8,128)} fusion(bf16[3072,1024]{1,0:T(8,128)(2,1)} %all-gather.3.cloned.1.call-done, f32[3072,256]{0,1:T(8,128)} %fusion.12, f32[3072,256]{0,1:T(8,128)} %fusion.9), kind=kOutput, calls=%fused_computation.11 | convolution fusion | flops 1615331328 | bytes 13631488 | tf_op jit(solution)/shard_map/dot_general | solution.py:11
  248.8 5.7 %convolution_bitcast_fusion.1 = f32[1,1024,256]{2,1,0:T(8,128)} fusion(bf16[3072,1024]{1,0:T(8,128)(2,1)} %all-gather.5.cloned.1.call-done, bf16[3072,256]{0,1:T(8,128)(2,1)S(1)} %get-tuple-element.10), kind=kOutput, calls=%fused_computation.13 | convolution fusion | flops 1610612736 | bytes 8912896 | tf_op jit(solution)/shard_map/dot_general | solution.py:11
  254.5 21.2 %reduce-scatter.2.cloned.1.call-done = bf16[384,1024]{1,0:T(8,128)(2,1)} async-done(((bf16[3072,1024]{1,0:T(8,128)(2,1)}), bf16[384,1024]{1,0:T(8,128)(2,1)}) %reduce-scatter.2.cloned.1.call-update) | async-done | bytes 786448 | tf_op jit(solution)/shard_map/reduce_scatter | solution.py:67
  275.6 2.1 all_to_all.36
  277.8 7.6 %all-to-all-start.2 = ((bf16[32,12,1024]{2,1,0:T(8,128)(2,1)}), bf16[32,12,1024]{2,1,0:T(8,128)(2,1)S(1)}, u32[]{:S(2)}, u32[]{:S(2)}) async-start(bf16[32,12,1024]{2,1,0:T(8,128)(2,1)} %all_to_all.36), calls=%async_computation.3 | async-start | bytes 2097152 | tf_op jit(solution)/shard_map/all_to_all | solution.py:59
  285.4 5.6 %convolution_bitcast_fusion = f32[1,1024,256]{2,1,0:T(8,128)} fusion(bf16[3072,1024]{1,0:T(8,128)(2,1)} %all-gather.5.cloned.1.call-done, bf16[3072,256]{0,1:T(8,128)(2,1)S(1)} %copy-done.2), kind=kOutput, calls=%fused_computation.12 | convolution fusion | flops 1610612736 | bytes 8912896 | tf_op jit(solution)/shard_map/dot_general | solution.py:11
  291.0 0.5 broadcast.24
  291.5 0.7 reduce.3
  292.2 0.1 broadcast_in_dim.62
  292.3 0.1 select_reduce_fusion.1
  292.4 0.6 maximum_divide_fusion
  293.0 9.4 %all-to-all-done.2 = bf16[32,12,1024]{2,1,0:T(8,128)(2,1)S(1)} async-done(((bf16[32,12,1024]{2,1,0:T(8,128)(2,1)}), bf16[32,12,1024]{2,1,0:T(8,128)(2,1)S(1)}, u32[]{:S(2)}, u32[]{:S(2)}) %all-to-all-start.2) | async-done | bytes 786464 | tf_op jit(solution)/shard_map/all_to_all | solution.py:59
  302.4 0.2 all_to_all.38
  302.6 1.0 convolution_convert_fusion.2
  (16 shorter events, 0.0 us)
Async XLA Ops:
  7.2 103.2 %copy-start = (bf16[1,1024,256]{2,1,0:T(8,128)(2,1)S(1)}, bf16[1,1024,256]{2,1,0:T(8,128)(2,1)}, u32[]{:S(2)}) copy-start(bf16[1,1024,256]{2,1,0:T(8,128)(2,1)} %param.11) | copy-start | bytes 1572868
  7.2 103.2 %all-gather.5.cloned.1.call-start = ((), (), s32[]{:S(2)}) async-start(), calls=%async_computation.6 | async-start | bytes 7077888 | tf_op jit(solution)/shard_map/all_gather | solution.py:61
  10.2 26.8 %copy-start.5 = (f32[128,2]{0,1:T(2,128)S(1)}, f32[128,2]{0,1:T(2,128)}, u32[]{:S(2)}) copy-start(f32[128,2]{0,1:T(2,128)} %param.10) | copy-start | bytes 3076
  10.2 26.8 %copy-start.4 = (bf16[128,1024]{1,0:T(8,128)(2,1)S(1)}, bf16[128,1024]{1,0:T(8,128)(2,1)}, u32[]{:S(2)}) copy-start(bf16[128,1024]{1,0:T(8,128)(2,1)} %param.8) | copy-start | bytes 786436
  36.9 148.9 %all-gather.3.cloned.1.call-start = ((), (), s32[]{:S(2)}) async-start(), calls=%async_computation.5 | async-start | bytes 7077888 | tf_op jit(solution)/shard_map/all_gather | solution.py:62
  59.3 57.5 %copy-start.3 = (bf16[1,1024,256]{2,1,0:T(8,128)(2,1)S(1)}, bf16[1,1024,256]{2,1,0:T(8,128)(2,1)}, u32[]{:S(2)}) copy-start(bf16[1,1024,256]{2,1,0:T(8,128)(2,1)} %param.12) | copy-start | bytes 1572868
  59.3 216.3 %reduce-scatter.2.cloned.1.call-start = ((), (), s32[]{:S(2)}) async-start(), calls=%async_computation.7 | async-start | bytes 7077888 | tf_op jit(solution)/shard_map/reduce_scatter | solution.py:67
  110.4 6.4 %copy-start.6 = (bf16[3072,1024]{1,0:T(8,128)(2,1)S(1)}, bf16[3072,1024]{1,0:T(8,128)(2,1)}, u32[]{:S(2)}) copy-start(bf16[3072,1024]{1,0:T(8,128)(2,1)} %all-gather.5.cloned.1.call-done) | copy-start | bytes 18874372
  116.8 69.0 %copy-start.7 = (bf16[1,256,1024]{2,1,0:T(8,128)(2,1)S(1)}, bf16[1,256,1024]{2,1,0:T(8,128)(2,1)}, u32[]{:S(2)}) copy-start(bf16[1,256,1024]{2,1,0:T(8,128)(2,1)} %param.13) | copy-start | bytes 1572868
  194.8 1.9 copy-start.1
  201.2 0.7 copy-start.8
  227.2 50.6 %all-to-all-start.3 = ((f32[32,12,1]{1,2,0:T(1,128)}), f32[32,12,1]{1,2,0:T(1,128)S(1)}, u32[]{:S(2)}, u32[]{:S(2)}) async-start(f32[32,12,1]{1,2,0:T(1,128)} %bitcast.13), calls=%async_computation.4 | async-start | bytes 32768 | tf_op jit(solution)/shard_map/all_to_all | solution.py:59
  254.5 30.9 %copy-start.2 = (bf16[3072,256]{0,1:T(8,128)(2,1)S(1)}, bf16[3072,256]{0,1:T(8,128)(2,1)}, u32[]{:S(2)}) copy-start(bf16[3072,256]{0,1:T(8,128)(2,1)} %copy-done.1) | copy-start | bytes 4718596
  277.8 24.6 %all-to-all-start.2 = ((bf16[32,12,1024]{2,1,0:T(8,128)(2,1)}), bf16[32,12,1024]{2,1,0:T(8,128)(2,1)S(1)}, u32[]{:S(2)}, u32[]{:S(2)}) async-start(bf16[32,12,1024]{2,1,0:T(8,128)(2,1)} %all_to_all.36), calls=%async_computation.3 | async-start | bytes 2097152 | tf_op jit(solution)/shard_map/all_to_all | solution.py:59
Sparse Core Ops, SparseCore 0:
  37.0 73.3 all-gather.4
  112.8 73.0 all-gather.2
  201.3 74.2 reduce-scatter.1
